TPU v7x, 256 devices: a whole 4x4x8 slice. The times are simulated.
256 devices in a mesh: grp: 4 (over y), slab: 64 (over z, x, core).
Axes of the slice: x: 4, y: 4, z: 8, core: 2. Of those that a mesh axis runs over, the one named last changes fastest.
Arguments:
- velocity: float32 [16, 3, 4, 131072], P(None, None, 'grp', 'slab'), may hold values from -6 to 6
- old_basis: bfloat16 [64, 3, 4, 131072], P(None, None, None, 'slab'), may hold values from -6 to 6
- singular_values: float32 [64], replicated, may hold values from 0.7 to 1.4
- thickness: int32 [4, 64], P('grp', 'slab'), may hold values from 1 to 4, as said below
Outputs:
- gram_matrix: float32 [80, 80], replicated
- new_basis: bfloat16 [64, 3, 4, 131072], P(None, None, None, 'slab')
- offsets: int32 [4, 64], P('grp', 'slab')
Inputs may be any that keep to these rules, and one draw needn't show every extreme that they name: `thickness`: the entry at row-major position p differs from 1 + (p * 3) // 256 by at most one. The first entry is 1 and the last is 4.
All inputs are finite; a program needn't handle non-finite values.
Results may differ from a plain program's by a relative error of at most 0.0004.
The roundings to bfloat16 on the way count: a program that leaves them out, or rounds other values in their place, can miss the bound.
Values may be sent and summed in bfloat16 or wider, within the bound.
No kernel may reach another device: no remote copies, remote signals or barrier semaphores. Data moves between devices by JAX's collectives and lax.ppermute only.
A program may use at most 64 MiB of HBM per device.

v0:
```python
import jax
import jax.numpy as jnp
from jax import lax
from jax.experimental import pallas as pl
from jax.experimental.pallas import tpu as pltpu
from jax.sharding import Mesh
from jax.sharding import PartitionSpec as P


PLANE = 512
SLAB = ("slab_0", "slab_1", "slab_2")

R = 64
S = 16
N = R + S
G = 4
COLS = 6144
J = 48
ROWS = 192
VPITCH = J + 8
PITCH = ROWS + 1
WIDE = (R + 1) * PITCH + 7
HIGHEST = lax.Precision.HIGHEST
MIB = 2**20


def vmem(n=1):
    return [pl.BlockSpec(memory_space=pltpu.VMEM) for _ in range(n)]


def smem():
    return pl.BlockSpec(memory_space=pltpu.SMEM)


def hbm(n=1):
    return [pl.BlockSpec(memory_space=pltpu.HBM) for _ in range(n)]


def near(x):
    return pltpu.with_memory_space_constraint(x, pltpu.VMEM)


def far(x):
    return pltpu.with_memory_space_constraint(x, pltpu.HBM)


def live_tile(t, thick, rows):
    return jnp.full((rows, 128), jnp.where(t // 4 < thick, 1, 0), jnp.int32) > 0


def snapshots_body(vel_hbm, snap_ref, vel_ref, sem):
    get = pltpu.make_async_copy(vel_hbm, vel_ref.at[:, 0:J], sem)
    get.start()
    get.wait()
    rows_ref = vel_ref.reshape(S * VPITCH, 128)
    for j in range(J):
        rows = rows_ref[pl.ds(j, S, stride=VPITCH), :]
        snap_ref[:, pl.ds(j * 128, 128)] = rows.astype(jnp.bfloat16)


def snapshots(velocity):
    return pl.pallas_call(
        snapshots_body,
        out_shape=pltpu.VMEM((S, COLS), jnp.bfloat16),
        in_specs=hbm(),
        out_specs=vmem()[0],
        scratch_shapes=[pltpu.VMEM((S, VPITCH, 128), jnp.float32), pltpu.SemaphoreType.DMA(())],
        compiler_params=pltpu.CompilerParams(vmem_limit_bytes=2 * MIB),
        cost_estimate=pl.CostEstimate(flops=10**9, transcendentals=0, bytes_accessed=10**6),
        name="snapshots",
    )(far(velocity.reshape(S, J, 128)))


def gram_body(thick_ref, basis_ref, snap_ref, part_hbm, wide_ref, part_ref, sems):
    g = lax.axis_index("grp")
    core = lax.axis_index("slab_2")
    place = ((g * 8 + lax.axis_index("slab_0")) * 4 + lax.axis_index("slab_1")) * 2 + core
    thick = thick_ref[0, 0]

    def widen(r, _):
        wide_ref[pl.ds(r * PITCH, ROWS), :] = basis_ref[r].astype(jnp.float32)
        return 0

    lax.fori_loop(0, R, widen, 0, unroll=4)
    gram = jnp.zeros((N, N), jnp.float32)
    for lo in range(0, J, 48):
        parts = []
        for j in range(lo, lo + 48):
            rows = wide_ref[pl.ds(j * G + g, R, stride=PITCH), :].astype(jnp.bfloat16)
            both = jnp.concatenate([rows, snap_ref[:, pl.ds(j * 128, 128)]], 0)
            parts.append(jnp.where(live_tile(j % 16, thick, N), both, jnp.zeros((), jnp.bfloat16)))
        stacked = jnp.concatenate(parts, 1)
        gram += lax.dot_general(
            stacked, stacked, (((1,), (1,)), ((), ())), preferred_element_type=jnp.float32
        )
    gram = jnp.concatenate([gram, jnp.zeros((N, 128 - N), jnp.float32)], 1)
    lane = lax.broadcasted_iota(jnp.int32, (16, 128), 1)
    row = lax.broadcasted_iota(jnp.int32, (16, 128), 0)
    thick_block = jnp.where(row * 16 + lane == place, thick.astype(jnp.float32), 0.0)
    upper = jnp.where(lane < 80, gram[0:16], pltpu.roll(gram[32:48], 48, 1))
    last = jnp.where(lane < 112, pltpu.roll(gram[48:64], 32, 1), pltpu.roll(gram[64:80], 48, 1))
    lower = jnp.where(lane < 16, thick_block, jnp.where(lane < 80, gram[16:32], last))
    part_ref[0:16] = upper
    part_ref[16:32] = lower
    puts = [pltpu.make_async_copy(part_ref, part_hbm.at[i], sems.at[i]) for i in range(8)]
    for put in puts:
        put.start()
    for put in puts:
        put.wait()


def gram_partial(thickness, basis, snap):
    return pl.pallas_call(
        gram_body,
        out_shape=pltpu.HBM((8, 32, 128), jnp.float32),
        in_specs=[smem()] + vmem(2),
        out_specs=hbm()[0],
        scratch_shapes=[
            pltpu.VMEM((WIDE, 128), jnp.float32),
            pltpu.VMEM((32, 128), jnp.float32),
            pltpu.SemaphoreType.DMA((8,)),
        ],
        compiler_params=pltpu.CompilerParams(vmem_limit_bytes=16 * MIB),
        cost_estimate=pl.CostEstimate(flops=10**9, transcendentals=0, bytes_accessed=10**7),
        name="gram",
    )(thickness, near(basis), near(snap))


def tree_sum(pieces):
    while len(pieces) > 1:
        pieces = [sum(pieces[i + 1 : i + 2], pieces[i]) for i in range(0, len(pieces), 2)]
    return pieces[0]


def combine_body(*refs):
    *ins, out_ref = refs
    pieces = [ref[i] for ref in ins for i in range(ref.shape[0])]
    total = tree_sum(pieces)
    for i in range(out_ref.shape[0]):
        out_ref[i] = total


def combine(arrays, copies):
    return pl.pallas_call(
        combine_body,
        out_shape=pltpu.VMEM((copies, 32, 128), jnp.float32),
        in_specs=vmem(len(arrays)),
        out_specs=vmem()[0],
        compiler_params=pltpu.CompilerParams(vmem_limit_bytes=MIB),
        name="combine",
    )(*(near(a) for a in arrays))


def whole_sum(x):
    return jnp.sum(x, keepdims=True)


def update_body(total_ref, sv_ref, basis_ref, s0, s1, s2, s3, gram_hbm, new_ref, off_hbm, snap_ref, wide_ref, f_ref, out_ref, gram_ref, off_ref, sems):
    g = lax.axis_index("grp")
    core = lax.axis_index("slab_2")
    slab = (lax.axis_index("slab_0") * 4 + lax.axis_index("slab_1")) * 2 + core
    place = g * 64 + slab
    gets = [
        pltpu.make_async_copy(ref, snap_ref.at[g ^ k], sems.at[12 + k])
        for k, ref in enumerate((s0, s1, s2, s3))
    ]
    for get in gets:
        get.start()
    upper, lower = total_ref[0, 0:16], total_ref[0, 16:32]
    lane = lax.broadcasted_iota(jnp.int32, (16, 128), 1)
    row = lax.broadcasted_iota(jnp.int32, (16, 128), 0)
    order = row * 16 + lane
    thick = jnp.where(lane < 16, lower, 0.0)
    off_ref[...] = whole_sum(jnp.where(order < place, thick, 0.0)).astype(jnp.int32)
    put_off = pltpu.make_async_copy(off_ref, off_hbm, sems.at[17])
    put_off.start()
    live = whole_sum(thick) * PLANE
    blocks = (
        upper,
        lower,
        pltpu.roll(upper, 128 - 48, 1),
        pltpu.roll(lower, 128 - 32, 1),
        pltpu.roll(lower, 128 - 48, 1),
    )
    diag = [jnp.where((lane >= 16 * i) & (lane < 80), b, 0.0) for i, b in enumerate(blocks)]
    strict = [jnp.where(lane >= 16 * (i + 1), b, 0.0) for i, b in enumerate(diag)]
    pad = [jnp.zeros((48, 128), jnp.float32)]
    raw = jnp.concatenate(diag + pad, 0) + jnp.concatenate(strict + pad, 0).T
    scale_row = jnp.concatenate([sv_ref[...], jnp.ones((1, 128 - R), jnp.float32)], 1)
    scale_cols = jnp.broadcast_to(scale_row, (128, 128))
    scale_rows = scale_cols.T
    full = raw * scale_rows * scale_cols / (3.0 * live)
    gram_ref[...] = full[:N, :N]
    put_gram = pltpu.make_async_copy(gram_ref, gram_hbm, sems.at[16])
    put_gram.start()
    it = full[:R]
    it = it * (0.5 * R**0.5 / jnp.sqrt(whole_sum(it * it)))
    for i in range(4):
        if i == 3:
            for get in gets:
                get.wait()
        for r in range(i * 16, i * 16 + 16):
            wide_ref[pl.ds(r * PITCH, ROWS), :] = basis_ref[r].astype(jnp.float32)
        prod = lax.dot_general(it, it, (((1,), (1,)), ((), ())), precision=HIGHEST)
        it = 1.5 * it - 0.5 * jnp.dot(prod, it, precision=HIGHEST)
    mix = (it * scale_cols[:R])[:, :N].astype(jnp.bfloat16)
    slab_thick = [
        whole_sum(jnp.where(order == k * 64 + slab, thick, 0.0)) for k in range(G)
    ]
    slab_live = [[jnp.broadcast_to(n, (R, 128)) > p for p in range(4)] for n in slab_thick]
    copies = []

    def compute(lo, hi):
        tiles = range(lo, hi)
        for k in range(G):
            parts = [wide_ref[pl.ds(j * G + k, R, stride=PITCH), :].astype(jnp.bfloat16) for j in tiles]
            snap = snap_ref[k, :, pl.ds(lo * 128, (hi - lo) * 128)]
            stacked = jnp.concatenate([jnp.concatenate(parts, 1), snap], 0)
            res = jnp.dot(mix, stacked, preferred_element_type=jnp.float32)
            for t, j in enumerate(tiles):
                part = jnp.where(slab_live[k][j % 16 // 4], res[:, t * 128 : (t + 1) * 128], 0.0)
                f_ref[pl.ds(j * G + k, R, stride=PITCH), :] = part

    def emit(lo, hi):
        at, rows = lo * G, (hi - lo) * G
        for r in range(R):
            out_ref[r, pl.ds(at, rows), :] = f_ref[pl.ds(r * PITCH + at, rows), :].astype(jnp.bfloat16)
        part = pl.ds(at, rows)
        copy = pltpu.make_async_copy(out_ref.at[:, part], new_ref.at[:, part], sems.at[len(copies)])
        copy.start()
        copies.append(copy)

    compute(0, 4)
    compute(4, 8)
    emit(0, 4)
    compute(8, 12)
    emit(4, 8)
    compute(12, 16)
    emit(8, 12)
    compute(16, 20)
    emit(12, 16)
    compute(20, 24)
    emit(16, 20)
    compute(24, 28)
    emit(20, 24)
    compute(28, 32)
    emit(24, 28)
    compute(32, 36)
    emit(28, 32)
    compute(36, 40)
    emit(32, 36)
    compute(40, 44)
    emit(36, 40)
    compute(44, 48)
    emit(40, 44)
    emit(44, 48)
    for copy in copies + [put_gram, put_off]:
        copy.wait()


def update(total, sv, basis, snaps):
    return pl.pallas_call(
        update_body,
        out_shape=(
            jax.ShapeDtypeStruct((N, N), jnp.float32),
            jax.ShapeDtypeStruct((R, ROWS, 128), jnp.bfloat16),
            jax.ShapeDtypeStruct((1, 1), jnp.int32),
        ),
        in_specs=vmem(3) + hbm(4),
        out_specs=[pl.BlockSpec(memory_space=pl.ANY) for _ in range(3)],
        scratch_shapes=[
            pltpu.VMEM((G, S, COLS), jnp.bfloat16),
            pltpu.VMEM((WIDE, 128), jnp.float32),
            pltpu.VMEM((WIDE, 128), jnp.float32),
            pltpu.VMEM((R, ROWS, 128), jnp.bfloat16),
            pltpu.VMEM((N, N), jnp.float32),
            pltpu.VMEM((1, 1), jnp.int32),
            pltpu.SemaphoreType.DMA((18,)),
        ],
        compiler_params=pltpu.CompilerParams(vmem_limit_bytes=28 * MIB),
        name="update",
    )(near(total), near(sv.reshape(1, R)), near(basis), *(far(s) for s in snaps))


def from_region(snap, k):
    return lax.ppermute(snap, "grp", [(i, i ^ k) for i in range(G)])


def per_device(velocity, old_basis, singular_values, thickness):
    basis = old_basis.reshape(R, 3, G, 16, 128).transpose(0, 1, 3, 2, 4).reshape(R, ROWS, 128)
    snap = snapshots(velocity)
    thickness = lax.optimization_barrier((thickness, snap))[0]
    snaps = [snap] + [from_region(snap, k) for k in (1, 2, 3)]
    part = gram_partial(thickness, basis, snap)
    got = lax.all_to_all(part, "slab_0", 0, 0, tiled=True)
    mine = combine((got,), 1)
    other = lax.ppermute(mine, "slab_2", [(0, 1), (1, 0)])
    spread = combine((mine, other), 16)
    got = lax.all_to_all(spread, ("grp", "slab_1"), 0, 0, tiled=True)
    total = combine((got,), 1)
    gram_matrix, new, offsets = update(total, singular_values, basis, snaps)
    new_basis = new.reshape(R, 3, 16, G, 128).transpose(0, 1, 3, 2, 4).reshape(R, 3, G, 2048)
    return (gram_matrix, new_basis, offsets)


def solution(mesh):
    split = Mesh(
        mesh.devices.reshape(mesh.shape["grp"], 8, 4, 2), ("grp", "slab_0", "slab_1", "slab_2")
    )
    in_specs = (P(None, None, "grp", SLAB), P(None, None, None, SLAB), P(), P("grp", SLAB))
    out_specs = (P(), P(None, None, None, SLAB), P("grp", SLAB))
    return jax.shard_map(
        per_device, mesh=split, in_specs=in_specs, out_specs=out_specs, check_vma=False
    )
```

profile of v0, /device:TPU:6, one launch (start us, length us, event | category | flops | bytes accessed | tf_op | source)
XLA Modules:
  0.0 50.6 jit_solution(280559351996987476)
XLA Ops:
  0.6 0.0 copy-start
  1.4 1.2 %snapshots.1.snap_ref.s0 = bf16[16,6144]{1,0:T(8,128)(2,1)S(1)} custom-call(f32[16,48,128]{2,1,0:T(8,128)} %bitcast.16), custom_call_target="tpu_custom_call" | custom-call | flops 1000000000 | bytes 1000000 | tf_op jit(solution)/shard_map/snapshots/pallas_call | solution.py:62
  2.7 0.0 copy-start.2
  2.7 0.0 copy-start.3
  2.7 0.0 copy-done
  2.7 1.7 %gram.1 = f32[8,32,128]{2,1,0:T(8,128)} custom-call(s32[1,1]{1,0:T(1,128)S(6)} %copy.9.thick_ref, bf16[64,192,128]{2,1,0:T(8,128)(2,1)S(1)} %bitcast.12, bf16[16,6144]{1,0:T(8,128)(2,1)S(1)} %snapshots.1.snap_ref.s0), custom_call_target="tpu_custom_call" | custom-call | flops 1000000000 | bytes 10000000 | tf_op jit(solution)/shard_map/gram/pallas_call | solution.py:113
  4.4 17.6 %all_to_all.10.refs_0_ = f32[8,32,128]{2,1,0:T(8,128)S(1)} all-to-all(f32[8,32,128]{2,1,0:T(8,128)} %gram.1), channel_id=1, replica_groups=mesh['grp'=4,'slab_0'=8,'slab_1'=4,'slab_2'=2] {'slab_0'}, dimensions={0} | all-to-all | bytes 262144 | tf_op jit(solution)/shard_map/all_to_all | solution.py:295
  22.0 0.1 collective-permute-start
  22.1 0.0 copy-done.2
  22.1 1.2 %collective-permute-done.refs_1_ = f32[1,32,128]{2,1,0:T(8,128)S(1)} collective-permute-done((f32[1,32,128]{2,1,0:T(8,128)S(1)}, f32[1,32,128]{2,1,0:T(8,128)S(1)}, u32[]{:S(2)}, u32[]{:S(2)}) %collective-permute-start) | collective-permute-done | bytes 16416 | tf_op jit(solution)/shard_map/ppermute | solution.py:297
  23.3 0.0 copy-start.1
  23.3 0.7 %copy-done.1 = f32[16,32,128]{2,1,0:T(8,128)} copy-done((f32[16,32,128]{2,1,0:T(8,128)}, f32[16,32,128]{2,1,0:T(8,128)S(1)}, u32[]{:S(2)}) %copy-start.1) | copy-done | bytes 262168
  24.0 7.4 %all-to-all-start.1 = ((f32[16,32,128]{2,1,0:T(8,128)}), f32[16,32,128]{2,1,0:T(8,128)S(1)}, u32[]{:S(2)}, u32[]{:S(2)}) async-start(f32[16,32,128]{2,1,0:T(8,128)} %copy-done.1), calls=%async_computation.1 | async-start | bytes 524288 | tf_op jit(solution)/shard_map/all_to_all | solution.py:299
  31.4 2.7 %collective-permute-start.3 = (bf16[16,6144]{1,0:T(8,128)(2,1)}, bf16[16,6144]{1,0:T(8,128)(2,1)}, u32[]{:S(2)}, u32[]{:S(2)}) collective-permute-start(bf16[16,6144]{1,0:T(8,128)(2,1)} %copy-done.2), channel_id=1, source_target_pairs={{0,192},{64,128},{128,64},{192,0},{1,193},{65,129},{129,65},{193,1... | collective-permute-start | bytes 589832 | tf_op jit(solution)/shard_map/ppermute | solution.py:286
  34.1 0.9 %collective-permute-start.2 = (bf16[16,6144]{1,0:T(8,128)(2,1)}, bf16[16,6144]{1,0:T(8,128)(2,1)}, u32[]{:S(2)}, u32[]{:S(2)}) collective-permute-start(bf16[16,6144]{1,0:T(8,128)(2,1)} %copy-done.2), channel_id=1, source_target_pairs={{0,128},{64,192},{128,0},{192,64},{1,129},{65,193},{129,1},{193,65... | collective-permute-start | bytes 589832 | tf_op jit(solution)/shard_map/ppermute | solution.py:286
  34.9 0.6 %collective-permute-start.1 = (bf16[16,6144]{1,0:T(8,128)(2,1)}, bf16[16,6144]{1,0:T(8,128)(2,1)}, u32[]{:S(2)}, u32[]{:S(2)}) collective-permute-start(bf16[16,6144]{1,0:T(8,128)(2,1)} %copy-done.2), channel_id=1, source_target_pairs={{0,64},{64,0},{128,192},{192,128},{1,65},{65,1},{129,193},{193,129... | collective-permute-start | bytes 589832 | tf_op jit(solution)/shard_map/ppermute | solution.py:286
  35.5 2.6 %all-to-all-done.1.refs_0_ = f32[16,32,128]{2,1,0:T(8,128)S(1)} async-done(((f32[16,32,128]{2,1,0:T(8,128)}), f32[16,32,128]{2,1,0:T(8,128)S(1)}, u32[]{:S(2)}, u32[]{:S(2)}) %all-to-all-start.1) | async-done | bytes 262176 | tf_op jit(solution)/shard_map/all_to_all | solution.py:299
  38.2 7.9 %collective-permute-done.3.s3 = bf16[16,6144]{1,0:T(8,128)(2,1)} collective-permute-done((bf16[16,6144]{1,0:T(8,128)(2,1)}, bf16[16,6144]{1,0:T(8,128)(2,1)}, u32[]{:S(2)}, u32[]{:S(2)}) %collective-permute-start.3) | collective-permute-done | bytes 196640 | tf_op jit(solution)/shard_map/ppermute | solution.py:286
  46.1 0.0 collective-permute-done.2.s2
  46.1 0.0 collective-permute-done.1.s1
  46.1 0.0 copy-done.3
  46.1 4.5 %update.1 = (f32[80,80]{1,0:T(8,128)}, bf16[64,192,128]{2,1,0:T(8,128)(2,1)}, s32[1,1]{1,0:T(1,128)}) custom-call(f32[1,32,128]{2,1,0:T(8,128)S(1)} %combine.5.total_ref, f32[1,64]{1,0:T(1,128)S(1)} %bitcast.14, bf16[64,192,128]{2,1,0:T(8,128)(2,1)S(1)} %bitcast.13, bf16[16,6144]{1,0:T(8,128)(2,1)} %copy-done.2, bf16[16,6144]{1,0:T(8,128)(2,1)} %collective-permute-done.1.s1, ...), custom_call_target="tpu_custom_call" | custom-call | tf_op jit(solution)/shard_map/update/pallas_call | solution.py:262
  (3 shorter events, 0.1 us)
Async XLA Ops:
  0.6 2.1 %copy-start = (bf16[64,3,4,2048]{3,2,1,0:T(4,128)(2,1)S(1)}, bf16[64,3,4,2048]{3,2,1,0:T(4,128)(2,1)}, u32[]{:S(2)}) copy-start(bf16[64,3,4,2048]{3,2,1,0:T(4,128)(2,1)} %param.5) | copy-start | bytes 9437188
  2.7 19.4 %copy-start.2 = (bf16[16,6144]{1,0:T(8,128)(2,1)}, bf16[16,6144]{1,0:T(8,128)(2,1)S(1)}, u32[]{:S(2)}) copy-start(bf16[16,6144]{1,0:T(8,128)(2,1)S(1)} %snapshots.1.snap_ref.s0) | copy-start | bytes 589828
  2.7 43.4 %copy-start.3 = (f32[64]{0:T(128)S(1)}, f32[64]{0:T(128)}, u32[]{:S(2)}) copy-start(f32[64]{0:T(128)} %param.6) | copy-start | bytes 772
  22.0 1.3 %collective-permute-start = (f32[1,32,128]{2,1,0:T(8,128)S(1)}, f32[1,32,128]{2,1,0:T(8,128)S(1)}, u32[]{:S(2)}, u32[]{:S(2)}) collective-permute-start(f32[1,32,128]{2,1,0:T(8,128)S(1)} %combine.3.refs_0_), channel_id=1, source_target_pairs={{0,1},{1,0},{2,3},{3,2},{4,5},{5,4},{6,7},{7,6},{8,9},{9,8},{10,11... | collective-permute-start | bytes 49160 | tf_op jit(solution)/shard_map/ppermute | solution.py:297
  23.3 0.7 %copy-start.1 = (f32[16,32,128]{2,1,0:T(8,128)}, f32[16,32,128]{2,1,0:T(8,128)S(1)}, u32[]{:S(2)}) copy-start(f32[16,32,128]{2,1,0:T(8,128)S(1)} %combine.4) | copy-start | bytes 786436
  24.0 14.2 %all-to-all-start.1 = ((f32[16,32,128]{2,1,0:T(8,128)}), f32[16,32,128]{2,1,0:T(8,128)S(1)}, u32[]{:S(2)}, u32[]{:S(2)}) async-start(f32[16,32,128]{2,1,0:T(8,128)} %copy-done.1), calls=%async_computation.1 | async-start | bytes 524288 | tf_op jit(solution)/shard_map/all_to_all | solution.py:299
  31.4 14.7 %collective-permute-start.3 = (bf16[16,6144]{1,0:T(8,128)(2,1)}, bf16[16,6144]{1,0:T(8,128)(2,1)}, u32[]{:S(2)}, u32[]{:S(2)}) collective-permute-start(bf16[16,6144]{1,0:T(8,128)(2,1)} %copy-done.2), channel_id=1, source_target_pairs={{0,192},{64,128},{128,64},{192,0},{1,193},{65,129},{129,65},{193,1... | collective-permute-start | bytes 589832 | tf_op jit(solution)/shard_map/ppermute | solution.py:286
  34.1 12.0 %collective-permute-start.2 = (bf16[16,6144]{1,0:T(8,128)(2,1)}, bf16[16,6144]{1,0:T(8,128)(2,1)}, u32[]{:S(2)}, u32[]{:S(2)}) collective-permute-start(bf16[16,6144]{1,0:T(8,128)(2,1)} %copy-done.2), channel_id=1, source_target_pairs={{0,128},{64,192},{128,0},{192,64},{1,129},{65,193},{129,1},{193,65... | collective-permute-start | bytes 589832 | tf_op jit(solution)/shard_map/ppermute | solution.py:286
  34.9 11.2 %collective-permute-start.1 = (bf16[16,6144]{1,0:T(8,128)(2,1)}, bf16[16,6144]{1,0:T(8,128)(2,1)}, u32[]{:S(2)}, u32[]{:S(2)}) collective-permute-start(bf16[16,6144]{1,0:T(8,128)(2,1)} %copy-done.2), channel_id=1, source_target_pairs={{0,64},{64,0},{128,192},{192,128},{1,65},{65,1},{129,193},{193,129... | collective-permute-start | bytes 589832 | tf_op jit(solution)/shard_map/ppermute | solution.py:286
where the time goes:
time: 51.4 us; the launch traced here: 50.6 us
  blocking collectives  17.6 us (34%)
  waiting for transfers between devices  11.7 us (23%)
  starting transfers between devices  11.6 us (23%)
  Pallas kernels  7.45 us (14%)
  between operations  1.52 us (3%)
  local copies, waits for them, and re-layouts  0.71 us (1%)
    all_to_all x1, blocking collectives, per_device(): got = lax.all_to_all(part, 'slab_0', 0, 0, tiled=True)  17.6 us
    ppermute x3, waiting for transfers between devices, from_region(): return lax.ppermute(snap, 'grp', [(i, i ^ k) for i in range(G)])  7.92 us
    all_to_all x1, starting transfers between devices, per_device(): got = lax.all_to_all(spread, ('grp', 'slab_1'), 0, 0, tiled=True)  7.43 us
    pallas_call x1, Pallas kernels, update(): pl.pallas_call(update_body, out_shape=(jax.ShapeDtypeStruct((N, N), jnp.f...  4.48 us
    ppermute x3, starting transfers between devices, from_region(): return lax.ppermute(snap, 'grp', [(i, i ^ k) for i in range(G)])  4.09 us
    all_to_all x1, waiting for transfers between devices, per_device(): got = lax.all_to_all(spread, ('grp', 'slab_1'), 0, 0, tiled=True)  2.65 us
    pallas_call x1, Pallas kernels, gram_partial(): pl.pallas_call(gram_body, out_shape=pltpu.HBM((8, 32, 128), jnp.float32),...  1.67 us
    pallas_call x1, Pallas kernels, snapshots(): pl.pallas_call(snapshots_body, out_shape=pltpu.VMEM((S, COLS), jnp.bfloat...  1.24 us
  transfers between devices with their start and end apart: 5, of which 3 were waited for; matrix products, arithmetic and copies ran while one was open for 0% of the time, Pallas kernels for 0%

commit v1 on v0

--- a/solution.py
+++ b/solution.py
@@ -71,7 +71,7 @@
     )(far(velocity.reshape(S, J, 128)))
 
 
-def gram_body(thick_ref, basis_ref, snap_ref, part_hbm, wide_ref, part_ref, sems):
+def gram_body(thick_ref, basis_ref, snap_ref, part_ref, wide_ref, stack_ref):
     g = lax.axis_index("grp")
     core = lax.axis_index("slab_2")
     place = ((g * 8 + lax.axis_index("slab_0")) * 4 + lax.axis_index("slab_1")) * 2 + core
@@ -81,7 +81,7 @@
         wide_ref[pl.ds(r * PITCH, ROWS), :] = basis_ref[r].astype(jnp.float32)
         return 0
 
-    lax.fori_loop(0, R, widen, 0, unroll=4)
+    lax.fori_loop(0, R, widen, 0, unroll=16)
     gram = jnp.zeros((N, N), jnp.float32)
     for lo in range(0, J, 48):
         parts = []
@@ -100,26 +100,17 @@
     upper = jnp.where(lane < 80, gram[0:16], pltpu.roll(gram[32:48], 48, 1))
     last = jnp.where(lane < 112, pltpu.roll(gram[48:64], 32, 1), pltpu.roll(gram[64:80], 48, 1))
     lower = jnp.where(lane < 16, thick_block, jnp.where(lane < 80, gram[16:32], last))
-    part_ref[0:16] = upper
-    part_ref[16:32] = lower
-    puts = [pltpu.make_async_copy(part_ref, part_hbm.at[i], sems.at[i]) for i in range(8)]
-    for put in puts:
-        put.start()
-    for put in puts:
-        put.wait()
+    part_ref[0, 0:16] = upper
+    part_ref[0, 16:32] = lower
 
 
 def gram_partial(thickness, basis, snap):
     return pl.pallas_call(
         gram_body,
-        out_shape=pltpu.HBM((8, 32, 128), jnp.float32),
+        out_shape=pltpu.VMEM((1, 32, 128), jnp.float32),
         in_specs=[smem()] + vmem(2),
-        out_specs=hbm()[0],
-        scratch_shapes=[
-            pltpu.VMEM((WIDE, 128), jnp.float32),
-            pltpu.VMEM((32, 128), jnp.float32),
-            pltpu.SemaphoreType.DMA((8,)),
-        ],
+        out_specs=vmem()[0],
+        scratch_shapes=[pltpu.VMEM((WIDE, 128), jnp.float32), pltpu.VMEM((N, COLS), jnp.bfloat16)],
         compiler_params=pltpu.CompilerParams(vmem_limit_bytes=16 * MIB),
         cost_estimate=pl.CostEstimate(flops=10**9, transcendentals=0, bytes_accessed=10**7),
         name="gram",
@@ -292,10 +283,10 @@
     thickness = lax.optimization_barrier((thickness, snap))[0]
     snaps = [snap] + [from_region(snap, k) for k in (1, 2, 3)]
     part = gram_partial(thickness, basis, snap)
-    got = lax.all_to_all(part, "slab_0", 0, 0, tiled=True)
-    mine = combine((got,), 1)
-    other = lax.ppermute(mine, "slab_2", [(0, 1), (1, 0)])
-    spread = combine((mine, other), 16)
+    got = lax.ppermute(part, "slab_2", [(0, 1), (1, 0)])
+    spread = combine((part, got), 8)
+    got = lax.all_to_all(spread, "slab_0", 0, 0, tiled=True)
+    spread = combine((got,), 16)
     got = lax.all_to_all(spread, ("grp", "slab_1"), 0, 0, tiled=True)
     total = combine((got,), 1)
     gram_matrix, new, offsets = update(total, singular_values, basis, snaps)

time: 51.4 us -> 48.5 us (0.944)
  waiting for transfers between devices: 11.7 us -> 10 us
  Pallas kernels: 7.45 us -> 6.68 us
    ppermute x3, waiting for transfers between devices: 7.92 us -> 4.69 us  [from_region(): return lax.ppermute(snap, 'grp', [(i, i ^ k) for i in range(G)])]
    all_to_all x1, waiting for transfers between devices: 2.65 us -> 4.14 us  [per_device(): got = lax.all_to_all(spread, ('grp', 'slab_1'), 0, 0, tiled=True)]
    pallas_call x1, Pallas kernels: 1.67 us -> 0.91 us  [gram_partial(): pl.pallas_call(gram_body, out_shape=pltpu.VMEM((1, 32, 128), jnp.float32)...]
where the time goes in v1:
time: 48.5 us; the launch traced here: 48.1 us
  blocking collectives  17.7 us (36%)
  starting transfers between devices  11.6 us (24%)
  waiting for transfers between devices  10 us (21%)
  Pallas kernels  6.68 us (14%)
  between operations  1.5 us (3%)
  local copies, waits for them, and re-layouts  0.71 us (1%)
    all_to_all x1, blocking collectives, per_device(): got = lax.all_to_all(spread, 'slab_0', 0, 0, tiled=True)  17.7 us
    all_to_all x1, starting transfers between devices, per_device(): got = lax.all_to_all(spread, ('grp', 'slab_1'), 0, 0, tiled=True)  7.42 us
    ppermute x3, waiting for transfers between devices, from_region(): return lax.ppermute(snap, 'grp', [(i, i ^ k) for i in range(G)])  4.69 us
    pallas_call x1, Pallas kernels, update(): pl.pallas_call(update_body, out_shape=(jax.ShapeDtypeStruct((N, N), jnp.f...  4.48 us
    all_to_all x1, waiting for transfers between devices, per_device(): got = lax.all_to_all(spread, ('grp', 'slab_1'), 0, 0, tiled=True)  4.14 us
    ppermute x3, starting transfers between devices, from_region(): return lax.ppermute(snap, 'grp', [(i, i ^ k) for i in range(G)])  4.09 us
    pallas_call x1, Pallas kernels, snapshots(): pl.pallas_call(snapshots_body, out_shape=pltpu.VMEM((S, COLS), jnp.bfloat...  1.24 us
    ppermute x1, waiting for transfers between devices, per_device(): got = lax.ppermute(part, 'slab_2', [(0, 1), (1, 0)])  1.17 us
  transfers between devices with their start and end apart: 5, of which 3 were waited for; matrix products, arithmetic and copies ran while one was open for 0% of the time, Pallas kernels for 0%

profile of v1, /device:TPU:6, one launch (start us, length us, event | category | flops | bytes accessed | tf_op | source)
XLA Modules:
  0.0 48.1 jit_solution(9865255871054705568)
XLA Ops:
  0.6 0.0 copy-start
  1.4 1.2 %snapshots.1.snap_ref.s0 = bf16[16,6144]{1,0:T(8,128)(2,1)S(1)} custom-call(f32[16,48,128]{2,1,0:T(8,128)} %bitcast.16), custom_call_target="tpu_custom_call" | custom-call | flops 1000000000 | bytes 1000000 | tf_op jit(solution)/shard_map/snapshots/pallas_call | solution.py:62
  2.7 0.0 copy-start.2
  2.7 0.0 copy-start.3
  2.7 0.0 copy-done
  2.7 0.9 %gram.1.refs_0_ = f32[1,32,128]{2,1,0:T(8,128)S(1)} custom-call(s32[1,1]{1,0:T(1,128)S(6)} %copy.9.thick_ref, bf16[64,192,128]{2,1,0:T(8,128)(2,1)S(1)} %bitcast.12, bf16[16,6144]{1,0:T(8,128)(2,1)S(1)} %snapshots.1.snap_ref.s0), custom_call_target="tpu_custom_call" | custom-call | flops 1000000000 | bytes 10000000 | tf_op jit(solution)/shard_map/gram/pallas_call | solution.py:108
  3.6 0.0 collective-permute-start
  3.7 1.2 %collective-permute-done.refs_1_ = f32[1,32,128]{2,1,0:T(8,128)S(1)} collective-permute-done((f32[1,32,128]{2,1,0:T(8,128)S(1)}, f32[1,32,128]{2,1,0:T(8,128)S(1)}, u32[]{:S(2)}, u32[]{:S(2)}) %collective-permute-start) | collective-permute-done | bytes 16416 | tf_op jit(solution)/shard_map/ppermute | solution.py:286
  4.9 17.7 %all_to_all.10.refs_0_ = f32[8,32,128]{2,1,0:T(8,128)S(1)} all-to-all(f32[8,32,128]{2,1,0:T(8,128)S(1)} %combine.3), channel_id=1, replica_groups=mesh['grp'=4,'slab_0'=8,'slab_1'=4,'slab_2'=2] {'slab_0'}, dimensions={0} | all-to-all | bytes 262144 | tf_op jit(solution)/shard_map/all_to_all | solution.py:288
  22.5 0.0 copy-done.2
  22.6 0.0 copy-start.1
  22.6 0.7 %copy-done.1 = f32[16,32,128]{2,1,0:T(8,128)} copy-done((f32[16,32,128]{2,1,0:T(8,128)}, f32[16,32,128]{2,1,0:T(8,128)S(1)}, u32[]{:S(2)}) %copy-start.1) | copy-done | bytes 262168
  23.3 7.4 %all-to-all-start.1 = ((f32[16,32,128]{2,1,0:T(8,128)}), f32[16,32,128]{2,1,0:T(8,128)S(1)}, u32[]{:S(2)}, u32[]{:S(2)}) async-start(f32[16,32,128]{2,1,0:T(8,128)} %copy-done.1), calls=%async_computation.1 | async-start | bytes 524288 | tf_op jit(solution)/shard_map/all_to_all | solution.py:290
  30.7 2.7 %collective-permute-start.3 = (bf16[16,6144]{1,0:T(8,128)(2,1)}, bf16[16,6144]{1,0:T(8,128)(2,1)}, u32[]{:S(2)}, u32[]{:S(2)}) collective-permute-start(bf16[16,6144]{1,0:T(8,128)(2,1)} %copy-done.2), channel_id=1, source_target_pairs={{0,192},{64,128},{128,64},{192,0},{1,193},{65,129},{129,65},{193,1... | collective-permute-start | bytes 589832 | tf_op jit(solution)/shard_map/ppermute | solution.py:277
  33.4 0.9 %collective-permute-start.2 = (bf16[16,6144]{1,0:T(8,128)(2,1)}, bf16[16,6144]{1,0:T(8,128)(2,1)}, u32[]{:S(2)}, u32[]{:S(2)}) collective-permute-start(bf16[16,6144]{1,0:T(8,128)(2,1)} %copy-done.2), channel_id=1, source_target_pairs={{0,128},{64,192},{128,0},{192,64},{1,129},{65,193},{129,1},{193,65... | collective-permute-start | bytes 589832 | tf_op jit(solution)/shard_map/ppermute | solution.py:277
  34.2 0.6 %collective-permute-start.1 = (bf16[16,6144]{1,0:T(8,128)(2,1)}, bf16[16,6144]{1,0:T(8,128)(2,1)}, u32[]{:S(2)}, u32[]{:S(2)}) collective-permute-start(bf16[16,6144]{1,0:T(8,128)(2,1)} %copy-done.2), channel_id=1, source_target_pairs={{0,64},{64,0},{128,192},{192,128},{1,65},{65,1},{129,193},{193,129... | collective-permute-start | bytes 589832 | tf_op jit(solution)/shard_map/ppermute | solution.py:277
  34.8 4.1 %all-to-all-done.1.refs_0_ = f32[16,32,128]{2,1,0:T(8,128)S(1)} async-done(((f32[16,32,128]{2,1,0:T(8,128)}), f32[16,32,128]{2,1,0:T(8,128)S(1)}, u32[]{:S(2)}, u32[]{:S(2)}) %all-to-all-start.1) | async-done | bytes 262176 | tf_op jit(solution)/shard_map/all_to_all | solution.py:290
  38.9 4.7 %collective-permute-done.3.s3 = bf16[16,6144]{1,0:T(8,128)(2,1)} collective-permute-done((bf16[16,6144]{1,0:T(8,128)(2,1)}, bf16[16,6144]{1,0:T(8,128)(2,1)}, u32[]{:S(2)}, u32[]{:S(2)}) %collective-permute-start.3) | collective-permute-done | bytes 196640 | tf_op jit(solution)/shard_map/ppermute | solution.py:277
  43.6 0.0 collective-permute-done.2.s2
  43.6 0.0 collective-permute-done.1.s1
  43.6 0.0 copy-done.3
  43.6 4.5 %update.1 = (f32[80,80]{1,0:T(8,128)}, bf16[64,192,128]{2,1,0:T(8,128)(2,1)}, s32[1,1]{1,0:T(1,128)}) custom-call(f32[1,32,128]{2,1,0:T(8,128)S(1)} %combine.5.total_ref, f32[1,64]{1,0:T(1,128)S(1)} %bitcast.14, bf16[64,192,128]{2,1,0:T(8,128)(2,1)S(1)} %bitcast.13, bf16[16,6144]{1,0:T(8,128)(2,1)} %copy-done.2, bf16[16,6144]{1,0:T(8,128)(2,1)} %collective-permute-done.1.s1, ...), custom_call_target="tpu_custom_call" | custom-call | tf_op jit(solution)/shard_map/update/pallas_call | solution.py:253
  (3 shorter events, 0.1 us)
Async XLA Ops:
  0.6 2.1 %copy-start = (bf16[64,3,4,2048]{3,2,1,0:T(4,128)(2,1)S(1)}, bf16[64,3,4,2048]{3,2,1,0:T(4,128)(2,1)}, u32[]{:S(2)}) copy-start(bf16[64,3,4,2048]{3,2,1,0:T(4,128)(2,1)} %param.5) | copy-start | bytes 9437188
  2.7 19.8 %copy-start.2 = (bf16[16,6144]{1,0:T(8,128)(2,1)}, bf16[16,6144]{1,0:T(8,128)(2,1)S(1)}, u32[]{:S(2)}) copy-start(bf16[16,6144]{1,0:T(8,128)(2,1)S(1)} %snapshots.1.snap_ref.s0) | copy-start | bytes 589828
  2.7 40.9 %copy-start.3 = (f32[64]{0:T(128)S(1)}, f32[64]{0:T(128)}, u32[]{:S(2)}) copy-start(f32[64]{0:T(128)} %param.6) | copy-start | bytes 772
  3.6 1.2 %collective-permute-start = (f32[1,32,128]{2,1,0:T(8,128)S(1)}, f32[1,32,128]{2,1,0:T(8,128)S(1)}, u32[]{:S(2)}, u32[]{:S(2)}) collective-permute-start(f32[1,32,128]{2,1,0:T(8,128)S(1)} %gram.1.refs_0_), channel_id=1, source_target_pairs={{0,1},{1,0},{2,3},{3,2},{4,5},{5,4},{6,7},{7,6},{8,9},{9,8},{10,11... | collective-permute-start | bytes 49160 | tf_op jit(solution)/shard_map/ppermute | solution.py:286
  22.6 0.7 %copy-start.1 = (f32[16,32,128]{2,1,0:T(8,128)}, f32[16,32,128]{2,1,0:T(8,128)S(1)}, u32[]{:S(2)}) copy-start(f32[16,32,128]{2,1,0:T(8,128)S(1)} %combine.4) | copy-start | bytes 786436
  23.3 15.7 %all-to-all-start.1 = ((f32[16,32,128]{2,1,0:T(8,128)}), f32[16,32,128]{2,1,0:T(8,128)S(1)}, u32[]{:S(2)}, u32[]{:S(2)}) async-start(f32[16,32,128]{2,1,0:T(8,128)} %copy-done.1), calls=%async_computation.1 | async-start | bytes 524288 | tf_op jit(solution)/shard_map/all_to_all | solution.py:290
  30.7 12.9 %collective-permute-start.3 = (bf16[16,6144]{1,0:T(8,128)(2,1)}, bf16[16,6144]{1,0:T(8,128)(2,1)}, u32[]{:S(2)}, u32[]{:S(2)}) collective-permute-start(bf16[16,6144]{1,0:T(8,128)(2,1)} %copy-done.2), channel_id=1, source_target_pairs={{0,192},{64,128},{128,64},{192,0},{1,193},{65,129},{129,65},{193,1... | collective-permute-start | bytes 589832 | tf_op jit(solution)/shard_map/ppermute | solution.py:277
  33.4 10.3 %collective-permute-start.2 = (bf16[16,6144]{1,0:T(8,128)(2,1)}, bf16[16,6144]{1,0:T(8,128)(2,1)}, u32[]{:S(2)}, u32[]{:S(2)}) collective-permute-start(bf16[16,6144]{1,0:T(8,128)(2,1)} %copy-done.2), channel_id=1, source_target_pairs={{0,128},{64,192},{128,0},{192,64},{1,129},{65,193},{129,1},{193,65... | collective-permute-start | bytes 589832 | tf_op jit(solution)/shard_map/ppermute | solution.py:277
  34.2 9.4 %collective-permute-start.1 = (bf16[16,6144]{1,0:T(8,128)(2,1)}, bf16[16,6144]{1,0:T(8,128)(2,1)}, u32[]{:S(2)}, u32[]{:S(2)}) collective-permute-start(bf16[16,6144]{1,0:T(8,128)(2,1)} %copy-done.2), channel_id=1, source_target_pairs={{0,64},{64,0},{128,192},{192,128},{1,65},{65,1},{129,193},{193,129... | collective-permute-start | bytes 589832 | tf_op jit(solution)/shard_map/ppermute | solution.py:277
